TPU v7x, 256 devices: a 4x2x16 block of a 4x16x16 slice. The times are simulated.
256 devices in a mesh: groups: 2 (over y), seq: 128 (over z, x, core).
Axes of the slice: x: 4, y: 2, z: 16, core: 2. Of those that a mesh axis runs over, the one named last changes fastest.
The devices are a block of a 4x16x16 slice.
Arguments:
- queries: bfloat16 [65536, 2048], P(('groups', 'seq')), parts along dimension 0, may hold values from -20 to 20
- keys: bfloat16 [65536, 2048], P(('groups', 'seq')), parts along dimension 0, may hold values from -20 to 20
- values: bfloat16 [65536, 2048], P(('groups', 'seq')), parts along dimension 0, may hold values from -6 to 6
- block_counts: int32 [128], P('groups'), parts along dimension 0, may hold values from 2 to 6, as said below
- last_tokens: int32 [256], P('groups'), parts along dimension 0, may hold values from 64 to 128
- pack_order: int32 [256], P('groups'), parts along dimension 0, may hold values from 0 to 127, as said below
- decode_slot: int32 [128], P('groups'), parts along dimension 0, may hold values from 0 to 63, each once
Outputs:
- attended: bfloat16 [65536, 2048], P(('groups', 'seq')), parts along dimension 0
- cache_keys: bfloat16 [256, 256, 16, 128], P(('groups', 'seq')), parts along dimension 0
- cache_values: bfloat16 [256, 256, 16, 128], P(('groups', 'seq')), parts along dimension 0
There are 2 independent parts, one for each index of `groups`. A program takes and returns all parts, laid end to end along the dimension named above; each array names one. Nothing has to cross between parts.
Inputs may be any that keep to these rules, and one draw needn't show every extreme that they name: `block_counts`: they sum to 192; the largest equals 6. `pack_order`: each prompt number appears once. The last 1 positions hold null prompts, and the position before them a conditional prompt of 6 blocks. `decode_slot`: each slot appears once.
All inputs are finite; a program needn't handle non-finite values.
Results may differ from a plain program's by a relative error of at most 0.0034.
Values may be sent and summed in bfloat16 or wider, within the bound.
A program may use at most 64 MiB of HBM per device.

v0:
```python
import jax
import jax.numpy as jnp
from jax import lax
from jax.sharding import PartitionSpec as P

HEADS = 16
HEAD_DIM = 128
BLOCK = 128
MAXB = 6
MASKED_SCORE = -1e30


def shifted(block, axis, distance):
    devices = range(lax.axis_size(axis))
    route = [(i - distance, i) for i in devices if i - distance in devices]
    return lax.ppermute(block, axis, route)


def block_tables(block_counts, last_tokens, pack_order, decode_slot, total_blocks, block):
    pair_count = block_counts.shape[0]
    prompts = 2 * pair_count
    prompt_ids = jnp.arange(prompts, dtype=jnp.int32)
    prompt_sizes = jnp.concatenate([block_counts, jnp.ones((pair_count,), jnp.int32)])
    picked = (pack_order[:, None] == prompt_ids[None, :]).astype(jnp.int32)
    packed_sizes = jnp.sum(picked * prompt_sizes[None, :], axis=1)
    packed_tails = jnp.sum(picked * last_tokens[None, :], axis=1)
    block_ends = jnp.cumsum(packed_sizes)
    starts = block_ends - packed_sizes
    blocks = jnp.arange(total_blocks, dtype=jnp.int32)
    member = (
        (starts[None, :] <= blocks[:, None]) & (blocks[:, None] < block_ends[None, :])
    ).astype(jnp.int32)
    position = jnp.sum(member * prompt_ids[None, :], axis=1)
    prompt = jnp.sum(member * pack_order[None, :], axis=1)
    within = blocks - jnp.sum(member * starts[None, :], axis=1)
    is_last = blocks + 1 == jnp.sum(member * block_ends[None, :], axis=1)
    valid_tokens = jnp.where(is_last, jnp.sum(member * packed_tails[None, :], axis=1), block)
    pair_ids = jnp.arange(pair_count, dtype=jnp.int32)
    earlier = (decode_slot[None, :] < decode_slot[:, None]).astype(jnp.int32)
    slot_start = jnp.sum(earlier * (block_counts + 1)[None, :], axis=1)
    pair_of = prompt % pair_count
    owner = (pair_of[:, None] == pair_ids[None, :]).astype(jnp.int32)
    base_slot = jnp.sum(owner * slot_start[None, :], axis=1)
    own_count = jnp.sum(owner * block_counts[None, :], axis=1)
    destination = base_slot + jnp.where(prompt >= pair_count, own_count, within)
    hits = (destination[None, :] == blocks[:, None]).astype(jnp.int32)
    source = jnp.sum(hits * blocks[None, :], axis=1)
    return (position, valid_tokens, source)


def hand_off(paired, source, devices):
    tokens_here = paired.shape[1]
    blocks_here = tokens_here // BLOCK
    splits = devices // HEADS
    slice_len = BLOCK // splits
    outgoing = paired.reshape(2, blocks_here, splits, slice_len, HEADS, HEAD_DIM)
    outgoing = jnp.transpose(outgoing, (4, 2, 0, 1, 3, 5)).reshape(
        devices, 2, blocks_here, slice_len, HEAD_DIM
    )
    arrived = lax.all_to_all(outgoing, "seq", split_axis=0, concat_axis=2, tiled=True)
    ordered = jnp.take(arrived[0], source, axis=1)
    return (ordered[0][None], ordered[1][None])


def attend(queries, paired, position, valid_tokens, own_index, reach):
    tokens_here, features = queries.shape
    blocks_here = tokens_here // BLOCK
    pieces = [paired]
    for distance in range(1, reach + 1):
        needed = min(blocks_here, MAXB - 1 - (distance - 1) * blocks_here)
        tail_part = paired[:, tokens_here - needed * BLOCK :]
        pieces.insert(0, shifted(tail_part, "seq", distance))
    prior_count = MAXB - 1
    window = jnp.concatenate(pieces, axis=1)
    window_blocks = prior_count + blocks_here
    lead_blocks = reach * blocks_here
    padded_docs = jnp.concatenate([jnp.full((lead_blocks,), -1, jnp.int32), position])
    padded_valid = jnp.concatenate([jnp.zeros((lead_blocks,), jnp.int32), valid_tokens])
    first_block = own_index * blocks_here + lead_blocks - prior_count
    window_docs = lax.dynamic_slice_in_dim(padded_docs, first_block, window_blocks)
    window_valid = lax.dynamic_slice_in_dim(padded_valid, first_block, window_blocks)
    own_first = own_index * blocks_here
    query_docs = lax.dynamic_slice_in_dim(position, own_first, blocks_here)
    query_valid = lax.dynamic_slice_in_dim(valid_tokens, own_first, blocks_here)
    token_ids = jnp.arange(BLOCK, dtype=jnp.int32)
    key_docs = jnp.repeat(window_docs, BLOCK)
    key_limit = jnp.repeat(window_valid, BLOCK)
    key_tokens = jnp.tile(token_ids, window_blocks)
    key_order = jnp.arange(window_blocks * BLOCK, dtype=jnp.int32) - prior_count * BLOCK
    query_order = jnp.arange(tokens_here, dtype=jnp.int32)
    allowed = key_docs[None, :] == jnp.repeat(query_docs, BLOCK)[:, None]
    allowed = (
        allowed & (key_order[None, :] <= query_order[:, None]) & (key_tokens < key_limit)[None, :]
    )
    query_ok = jnp.tile(token_ids, blocks_here) < jnp.repeat(query_valid, BLOCK)
    score_scale = HEAD_DIM ** (-0.5)
    query_heads = jnp.moveaxis(queries.reshape(tokens_here, HEADS, HEAD_DIM), 1, 0)
    key_heads = jnp.moveaxis(window[0].reshape(-1, HEADS, HEAD_DIM), 1, 0)
    value_heads = jnp.moveaxis(window[1].reshape(-1, HEADS, HEAD_DIM), 1, 0)

    def one_head(operands):
        query_part, key_part, value_part = operands
        scores = (
            jnp.einsum("qd,kd->qk", query_part, key_part, preferred_element_type=jnp.float32)
            * score_scale
        )
        scores = jnp.where(allowed, scores, MASKED_SCORE)
        peak = jnp.max(scores, axis=1, keepdims=True)
        weights = jnp.exp(scores - peak)
        totals = jnp.sum(weights, axis=1, keepdims=True)
        mixed = jnp.dot(
            weights.astype(jnp.bfloat16), value_part, preferred_element_type=jnp.float32
        )
        return mixed / totals

    head_outputs = lax.map(one_head, (query_heads, key_heads, value_heads))
    merged = jnp.moveaxis(head_outputs, 0, 1).reshape(tokens_here, features)
    return jnp.where(query_ok[:, None], merged, 0.0).astype(jnp.bfloat16)


def local(queries, keys, values, block_counts, last_tokens, pack_order, decode_slot):
    devices = lax.axis_size("seq")
    own_index = lax.axis_index("seq")
    tokens_here = queries.shape[0]
    blocks_here = tokens_here // BLOCK
    reach = (MAXB + blocks_here - 2) // blocks_here
    position, valid_tokens, source = block_tables(
        block_counts, last_tokens, pack_order, decode_slot, blocks_here * devices, BLOCK
    )
    paired = jnp.stack([keys, values])
    attended = attend(queries, paired, position, valid_tokens, own_index, reach)
    cache_keys, cache_values = hand_off(paired, source, devices)
    return (attended, cache_keys, cache_values)


def solution(mesh):
    placed = (
        P(("groups", "seq"), None),
        P(("groups", "seq"), None),
        P(("groups", "seq"), None),
        P("groups"),
        P("groups"),
        P("groups"),
        P("groups"),
    )
    return jax.shard_map(
        local,
        mesh=mesh,
        in_specs=placed,
        out_specs=(
            P(("groups", "seq"), None),
            P(("groups", "seq"), None, None, None),
            P(("groups", "seq"), None, None, None),
        ),
        check_vma=False,
    )
```

profile of v0, /device:TPU:33, one launch (start us, length us, event | category | flops | bytes accessed | tf_op | source)
XLA Modules:
  0.0 243.1 jit_solution(12251069177310898664)
XLA Ops:
  0.6 1.6 copy.37
  2.2 0.5 copy.38
  2.8 1.5 pad_maximum_fusion
  4.3 5.6 %collective-permute-start.1 = (bf16[2,256,2048]{1,2,0:T(8,128)(2,1)}, bf16[2,256,2048]{1,2,0:T(8,128)(2,1)}, u32[]{:S(2)}, u32[]{:S(2)}) collective-permute-start(bf16[2,256,2048]{1,2,0:T(8,128)(2,1)} %pad_maximum_fusion), channel_id=1, source_target_pairs={{0,2},{1,3},{2,4},{3,5},{4,6},{5,7},{6,8},{7,9},{8,10},{9,11},{10,... | collective-permute-start | bytes 6291464 | tf_op jit(solution)/shard_map/ppermute | solution.py:16
  9.9 2.7 %collective-permute-start.2 = (bf16[2,256,2048]{1,2,0:T(8,128)(2,1)}, bf16[2,256,2048]{1,2,0:T(8,128)(2,1)}, u32[]{:S(2)}, u32[]{:S(2)}) collective-permute-start(bf16[2,256,2048]{1,2,0:T(8,128)(2,1)} %pad_maximum_fusion), channel_id=1, source_target_pairs={{0,1},{1,2},{2,3},{3,4},{4,5},{5,6},{6,7},{7,8},{8,9},{9,10},{10,1... | collective-permute-start | bytes 6291464 | tf_op jit(solution)/shard_map/ppermute | solution.py:16
  12.6 1.1 fusion.20
  13.7 4.3 %collective-permute-start = (bf16[2,128,2048]{1,2,0:T(8,128)(2,1)}, bf16[2,128,2048]{1,2,0:T(8,128)(2,1)}, u32[]{:S(2)}, u32[]{:S(2)}) collective-permute-start(bf16[2,128,2048]{1,2,0:T(8,128)(2,1)} %fusion.20), channel_id=1, source_target_pairs={{0,3},{1,4},{2,5},{3,6},{4,7},{5,8},{6,9},{7,10},{8,11},{9,12},{10... | collective-permute-start | bytes 3145736 | tf_op jit(solution)/shard_map/ppermute | solution.py:16
  18.7 1.9 copy.43
  20.6 28.4 %all-to-all-start = ((bf16[128,2,2,16,128]{4,3,2,1,0:T(8,128)(2,1)}), bf16[128,2,2,16,128]{4,3,2,1,0:T(8,128)(2,1)}, u32[]{:S(2)}, u32[]{:S(2)}) async-start(bf16[128,2,2,16,128]{4,3,2,1,0:T(8,128)(2,1)} %bitcast.84), calls=%async_computation | async-start | bytes 4194304 | tf_op jit(solution)/shard_map/all_to_all | solution.py:60
  50.7 2.3 copy.36
  53.2 62.3 %collective-permute-done = bf16[2,128,2048]{1,2,0:T(8,128)(2,1)} collective-permute-done((bf16[2,128,2048]{1,2,0:T(8,128)(2,1)}, bf16[2,128,2048]{1,2,0:T(8,128)(2,1)}, u32[]{:S(2)}, u32[]{:S(2)}) %collective-permute-start) | collective-permute-done | bytes 1048608 | tf_op jit(solution)/shard_map/ppermute | solution.py:16
  115.5 3.5 %maximum_maximum_fusion = bf16[2,896,2048]{1,2,0:T(8,128)(2,1)S(1)} fusion(bf16[1,256,2048]{1,2,0:T(8,128)(2,1)S(1)} %bitcast.82, bf16[1,256,2048]{1,2,0:T(8,128)(2,1)S(1)} %bitcast.79, bf16[2,256,2048]{1,2,0:T(8,128)(2,1)} %collective-permute-done.2, bf16[2,256,2048]{1,2,0:T(8,128)(2,1)} %collective-permute-done.1, ...), kind=kLoop, calls=%fused_computation.22 | loop fusion | flops 36700160 | bytes 14680064 | tf_op jit(solution)/shard_map/concatenate | solution.py:74
  119.0 3.6 %fusion.26 = (bf16[1,896,2048]{1,2,0:T(8,128)(2,1)}, bf16[1,896,2048]{1,2,0:T(8,128)(2,1)}) fusion(bf16[2,896,2048]{1,2,0:T(8,128)(2,1)S(1)} %maximum_maximum_fusion), kind=kLoop, calls=%fused_computation.71 | loop fusion | bytes 14680064 | tf_op jit(solution)/shard_map/slice | solution.py:99
  122.6 50.8 %while.11 = (s32[]{:T(128)}, bf16[16,256,128]{2,1,0:T(8,128)(2,1)S(1)}, bf16[16,256,128]{1,2,0:T(8,128)(2,1)}, bf16[16,896,128]{1,2,0:T(8,128)(2,1)}, bf16[16,89...) while((s32[]{:T(128)}, ...), condition=%wide.region_9.10_spmd.clone, body=%wide.region_6.0_spmd.clone.sunk | while | flops 119995904 | bytes 3424229 | solution.py:116
  122.6 1.5 fusion.35
  124.1 0.3 fusion.36
  124.4 1.3 fusion.37
  125.7 1.5 fusion.35
  127.3 0.3 fusion.36
  127.6 1.3 fusion.37
  128.9 1.5 fusion.35
  130.5 0.3 fusion.36
  130.8 1.3 fusion.37
  132.1 1.5 fusion.35
  133.6 0.3 fusion.36
  133.9 1.3 fusion.37
  135.3 1.5 fusion.35
  136.8 0.3 fusion.36
  137.1 1.3 fusion.37
  138.5 1.5 fusion.35
  140.0 0.3 fusion.36
  140.3 1.3 fusion.37
  141.6 1.5 fusion.35
  143.2 0.3 fusion.36
  143.5 1.3 fusion.37
  144.8 1.5 fusion.35
  146.3 0.3 fusion.36
  146.6 1.3 fusion.37
  148.0 1.5 fusion.35
  149.5 0.3 fusion.36
  149.8 1.3 fusion.37
  151.2 1.5 fusion.35
  152.7 0.3 fusion.36
  153.0 1.3 fusion.37
  154.3 1.5 fusion.35
  155.9 0.3 fusion.36
  156.2 1.3 fusion.37
  157.5 1.5 fusion.35
  159.0 0.3 fusion.36
  159.3 1.3 fusion.37
  160.7 1.5 fusion.35
  162.5 1.3 fusion.37
  163.9 1.5 fusion.35
  165.7 1.3 fusion.37
  167.0 1.5 fusion.35
  168.9 1.3 fusion.37
  170.2 1.5 fusion.35
  172.0 1.3 fusion.37
  173.4 1.2 fusion.19
  174.6 59.9 %all-to-all-done = bf16[128,2,2,16,128]{4,3,2,1,0:T(8,128)(2,1)} async-done(((bf16[128,2,2,16,128]{4,3,2,1,0:T(8,128)(2,1)}), bf16[128,2,2,16,128]{4,3,2,1,0:T(8,128)(2,1)}, u32[]{:S(2)}, u32[]{:S(2)}) %all-to-all-start) | async-done | bytes 2097184 | tf_op jit(solution)/shard_map/all_to_all | solution.py:60
  234.5 3.3 %copy.44 = bf16[1,2,128,2,16,128]{5,4,3,2,1,0:T(8,128)(2,1)} copy(bf16[1,2,128,2,16,128]{5,4,3,1,2,0:T(8,128)(2,1)} %bitcast.17) | data formatting | bytes 4194304 | tf_op jit(solution)/shard_map/all_to_all | solution.py:60
  237.8 2.7 %gather_fusion = bf16[256,2,16,128]{3,2,1,0:T(8,128)(2,1)S(1)} fusion(bf16[2,256,16,128]{3,2,1,0:T(8,128)(2,1)} %bitcast.83, s32[1024]{0:T(1024)S(1)} %pad_clamp_fusion), kind=kCustom, calls=%fused_computation | custom fusion | bytes 4195328 | tf_op jit(solution)/shard_map/jit(_take)/gather | solution.py:61
  240.5 0.9 select_bitcast_fusion
  241.4 1.7 slice_bitcast_fusion
  (47 shorter events, 3.7 us)
Async XLA Ops:
  0.6 1.6 copy-start.1
  4.3 13.7 %copy-start = (bf16[256,2048]{1,0:T(8,128)(2,1)S(1)}, bf16[256,2048]{1,0:T(8,128)(2,1)}, u32[]{:S(2)}) copy-start(bf16[256,2048]{1,0:T(8,128)(2,1)} %param.10) | copy-start | bytes 3145732
  4.3 111.2 %collective-permute-start.1 = (bf16[2,256,2048]{1,2,0:T(8,128)(2,1)}, bf16[2,256,2048]{1,2,0:T(8,128)(2,1)}, u32[]{:S(2)}, u32[]{:S(2)}) collective-permute-start(bf16[2,256,2048]{1,2,0:T(8,128)(2,1)} %pad_maximum_fusion), channel_id=1, source_target_pairs={{0,2},{1,3},{2,4},{3,5},{4,6},{5,7},{6,8},{7,9},{8,10},{9,11},{10,... | collective-permute-start | bytes 6291464 | tf_op jit(solution)/shard_map/ppermute | solution.py:16
  9.9 105.7 %collective-permute-start.2 = (bf16[2,256,2048]{1,2,0:T(8,128)(2,1)}, bf16[2,256,2048]{1,2,0:T(8,128)(2,1)}, u32[]{:S(2)}, u32[]{:S(2)}) collective-permute-start(bf16[2,256,2048]{1,2,0:T(8,128)(2,1)} %pad_maximum_fusion), channel_id=1, source_target_pairs={{0,1},{1,2},{2,3},{3,4},{4,5},{5,6},{6,7},{7,8},{8,9},{9,10},{10,1... | collective-permute-start | bytes 6291464 | tf_op jit(solution)/shard_map/ppermute | solution.py:16
  13.7 101.8 %collective-permute-start = (bf16[2,128,2048]{1,2,0:T(8,128)(2,1)}, bf16[2,128,2048]{1,2,0:T(8,128)(2,1)}, u32[]{:S(2)}, u32[]{:S(2)}) collective-permute-start(bf16[2,128,2048]{1,2,0:T(8,128)(2,1)} %fusion.20), channel_id=1, source_target_pairs={{0,3},{1,4},{2,5},{3,6},{4,7},{5,8},{6,9},{7,10},{8,11},{9,12},{10... | collective-permute-start | bytes 3145736 | tf_op jit(solution)/shard_map/ppermute | solution.py:16
  20.6 28.4 %copy-start.5 = (s32[64]{0:T(128)S(1)}, s32[64]{0:T(128)}, u32[]{:S(2)}) copy-start(s32[64]{0:T(128)} %param.12) | copy-start | bytes 772
  20.6 28.4 %copy-start.2 = (s32[128]{0:T(128)S(1)}, s32[128]{0:T(128)}, u32[]{:S(2)}) copy-start(s32[128]{0:T(128)} %param.14) | copy-start | bytes 1540
  20.6 28.4 %copy-start.4 = (s32[128]{0:T(128)S(1)}, s32[128]{0:T(128)}, u32[]{:S(2)}) copy-start(s32[128]{0:T(128)} %param.13) | copy-start | bytes 1540
  20.6 29.4 %copy-start.3 = (s32[64]{0:T(128)S(1)}, s32[64]{0:T(128)}, u32[]{:S(2)}) copy-start(s32[64]{0:T(128)} %param.15) | copy-start | bytes 772
  20.6 213.9 %all-to-all-start = ((bf16[128,2,2,16,128]{4,3,2,1,0:T(8,128)(2,1)}), bf16[128,2,2,16,128]{4,3,2,1,0:T(8,128)(2,1)}, u32[]{:S(2)}, u32[]{:S(2)}) async-start(bf16[128,2,2,16,128]{4,3,2,1,0:T(8,128)(2,1)} %bitcast.84), calls=%async_computation | async-start | bytes 4194304 | tf_op jit(solution)/shard_map/all_to_all | solution.py:60
where the time goes:
time: 244 us; the launch traced here: 243 us
  waiting for transfers between devices  122 us (50%)
  matrix products  45.6 us (19%)
  starting transfers between devices  41 us (17%)
  local copies, waits for them, and re-layouts  18.5 us (8%)
  other arithmetic  14.6 us (6%)
    ppermute x3, waiting for transfers between devices, shifted(): return lax.ppermute(block, axis, route)  62.3 us
    all_to_all x1, waiting for transfers between devices, hand_off(): lax.all_to_all(outgoing, 'seq', split_axis=0, concat_axis=2, tiled=True)  59.9 us
    all_to_all x1, starting transfers between devices, hand_off(): lax.all_to_all(outgoing, 'seq', split_axis=0, concat_axis=2, tiled=True)  28.4 us
    dot_general x16, matrix products, one_head(): jnp.einsum('qd,kd->qk', query_part, key_part, preferred_element_type=jnp....  24.4 us
    dot_general x16, matrix products, one_head(): jnp.dot(weights.astype(jnp.bfloat16), value_part, preferred_element_type=...  21.2 us
    ppermute x3, starting transfers between devices, shifted(): return lax.ppermute(block, axis, route)  12.6 us
    unnamed x18, local copies, waits for them, and re-layouts  6.51 us
  transfers between devices with their start and end apart: 4, of which 2 were waited for; matrix products, arithmetic and copies ran while one was open for 27% of the time, Pallas kernels for 0%

commit v1 on v0

--- a/solution.py
+++ b/solution.py
@@ -57,7 +57,10 @@
     outgoing = jnp.transpose(outgoing, (4, 2, 0, 1, 3, 5)).reshape(
         devices, 2, blocks_here, slice_len, HEAD_DIM
     )
-    arrived = lax.all_to_all(outgoing, "seq", split_axis=0, concat_axis=2, tiled=True)
+    arrived = jnp.concatenate(
+        lax.all_to_all(jnp.stack(jnp.split(outgoing, lax.axis_size("seq"), axis=0)), "seq", 0, 0),
+        axis=2,
+    )
     ordered = jnp.take(arrived[0], source, axis=1)
     return (ordered[0][None], ordered[1][None])
 

time: 244 us -> 233 us (0.955)
  waiting for transfers between devices: 122 us -> 35.5 us
  local copies, waits for them, and re-layouts: 18.5 us -> 94 us
    unnamed x18 -> x145, local copies, waits for them, and re-layouts: 6.51 us -> 82.7 us
    ppermute x3, waiting for transfers between devices: 62.3 us -> 0.01 us  [shifted(): return lax.ppermute(block, axis, route)]
    all_to_all x1, waiting for transfers between devices: 59.9 us -> 35.5 us  [hand_off(): lax.all_to_all(jnp.stack(jnp.split(outgoing, lax.axis_size('seq'), axis=0...]
    all_to_all x1 -> x0, local copies, waits for them, and re-layouts: 3.32 us -> none  [hand_off(): lax.all_to_all(outgoing, 'seq', split_axis=0, concat_axis=2, tiled=True)]
    reshape x0 -> x1, local copies, waits for them, and re-layouts: none -> 3.32 us  [hand_off(): jnp.concatenate(lax.all_to_all(jnp.stack(jnp.split(outgoing, lax.axis_siz...]
  transfers between devices with their start and end apart: 4 -> 4, of which waited for: 2 -> 1; matrix products, arithmetic and copies ran while one was open for 27% -> 61% of each run, Pallas kernels for 0% -> 0%
where the time goes in v1:
time: 233 us; the launch traced here: 232 us
  local copies, waits for them, and re-layouts  94 us (40%)
  matrix products  45.7 us (20%)
  starting transfers between devices  40.7 us (17%)
  waiting for transfers between devices  35.5 us (15%)
  other arithmetic  14.8 us (6%)
    unnamed x145, local copies, waits for them, and re-layouts  82.7 us
    all_to_all x1, waiting for transfers between devices, hand_off(): lax.all_to_all(jnp.stack(jnp.split(outgoing, lax.axis_size('seq'), axis=0...  35.5 us
    all_to_all x1, starting transfers between devices, hand_off(): lax.all_to_all(jnp.stack(jnp.split(outgoing, lax.axis_size('seq'), axis=0...  28.1 us
    dot_general x16, matrix products, one_head(): jnp.einsum('qd,kd->qk', query_part, key_part, preferred_element_type=jnp....  24.4 us
    dot_general x16, matrix products, one_head(): jnp.dot(weights.astype(jnp.bfloat16), value_part, preferred_element_type=...  21.3 us
    ppermute x3, starting transfers between devices, shifted(): return lax.ppermute(block, axis, route)  12.6 us
    reduce_sum x16, other arithmetic, one_head(): totals = jnp.sum(weights, axis=1, keepdims=True)  4.99 us
  transfers between devices with their start and end apart: 4, of which 1 were waited for; matrix products, arithmetic and copies ran while one was open for 61% of the time, Pallas kernels for 0%

profile of v1, /device:TPU:33, one launch (start us, length us, event | category | flops | bytes accessed | tf_op | source)
XLA Modules:
  0.0 232.0 jit_solution(1712068749454870083)
XLA Ops:
  0.6 1.6 copy.38
  2.8 1.5 pad_maximum_fusion
  4.3 4.7 %collective-permute-start.2 = (bf16[2,256,2048]{1,2,0:T(8,128)(2,1)}, bf16[2,256,2048]{1,2,0:T(8,128)(2,1)}, u32[]{:S(2)}, u32[]{:S(2)}) collective-permute-start(bf16[2,256,2048]{1,2,0:T(8,128)(2,1)} %pad_maximum_fusion), channel_id=1, source_target_pairs={{0,1},{1,2},{2,3},{3,4},{4,5},{5,6},{6,7},{7,8},{8,9},{9,10},{10,1... | collective-permute-start | bytes 6291464 | tf_op jit(solution)/shard_map/ppermute | solution.py:16
  9.0 4.6 %collective-permute-start.1 = (bf16[2,256,2048]{1,2,0:T(8,128)(2,1)}, bf16[2,256,2048]{1,2,0:T(8,128)(2,1)}, u32[]{:S(2)}, u32[]{:S(2)}) collective-permute-start(bf16[2,256,2048]{1,2,0:T(8,128)(2,1)} %pad_maximum_fusion), channel_id=1, source_target_pairs={{0,2},{1,3},{2,4},{3,5},{4,6},{5,7},{6,8},{7,9},{8,10},{9,11},{10,... | collective-permute-start | bytes 6291464 | tf_op jit(solution)/shard_map/ppermute | solution.py:16
  13.6 1.1 fusion.20
  14.7 3.3 %collective-permute-start = (bf16[2,128,2048]{1,2,0:T(8,128)(2,1)}, bf16[2,128,2048]{1,2,0:T(8,128)(2,1)}, u32[]{:S(2)}, u32[]{:S(2)}) collective-permute-start(bf16[2,128,2048]{1,2,0:T(8,128)(2,1)} %fusion.20), channel_id=1, source_target_pairs={{0,3},{1,4},{2,5},{3,6},{4,7},{5,8},{6,9},{7,10},{8,11},{9,12},{10... | collective-permute-start | bytes 3145736 | tf_op jit(solution)/shard_map/ppermute | solution.py:16
  21.1 0.6 constant_dynamic-update-slice_fusion.124
  30.0 0.6 constant_dynamic-update-slice_fusion.109
  30.7 0.6 constant_dynamic-update-slice_fusion.108
  34.3 0.6 constant_dynamic-update-slice_fusion.102
  34.9 0.6 constant_dynamic-update-slice_fusion.101
  37.3 0.6 constant_dynamic-update-slice_fusion.97
  45.1 0.6 constant_dynamic-update-slice_fusion.84
  49.3 0.6 constant_dynamic-update-slice_fusion.77
  54.7 0.6 constant_dynamic-update-slice_fusion.68
  61.3 0.6 constant_dynamic-update-slice_fusion.57
  68.5 0.6 constant_dynamic-update-slice_fusion.45
  73.9 0.6 constant_dynamic-update-slice_fusion.36
  78.1 0.6 constant_dynamic-update-slice_fusion.29
  81.1 0.6 constant_dynamic-update-slice_fusion.24
  90.1 0.6 constant_dynamic-update-slice_fusion.9
  96.2 28.1 %all-to-all-start = ((bf16[128,1,2,2,16,128]{5,4,3,2,1,0:T(8,128)(2,1)}), bf16[128,1,2,2,16,128]{5,4,3,2,1,0:T(8,128)(2,1)}, u32[]{:S(2)}, u32[]{:S(2)}) async-start(bf16[128,1,2,2,16,128]{5,4,3,2,1,0:T(8,128)(2,1)} %constant_dynamic-update-slice_fusion), calls=%async_computation | async-start | bytes 4194304 | tf_op jit(solution)/shard_map/all_to_all | solution.py:61
  126.0 2.3 copy.36
  128.5 3.5 %maximum_maximum_fusion = bf16[2,896,2048]{1,2,0:T(8,128)(2,1)S(1)} fusion(bf16[1,256,2048]{1,2,0:T(8,128)(2,1)S(1)} %bitcast.589, bf16[1,256,2048]{1,2,0:T(8,128)(2,1)S(1)} %bitcast.592, bf16[2,256,2048]{1,2,0:T(8,128)(2,1)} %collective-permute-done.2, bf16[2,256,2048]{1,2,0:T(8,128)(2,1)} %collective-permute-done.1, ...), kind=kLoop, calls=%fused_computation.22 | loop fusion | flops 36700160 | bytes 14680064 | tf_op jit(solution)/shard_map/concatenate | solution.py:77
  132.0 3.6 %fusion.26 = (bf16[1,896,2048]{1,2,0:T(8,128)(2,1)}, bf16[1,896,2048]{1,2,0:T(8,128)(2,1)}) fusion(bf16[2,896,2048]{1,2,0:T(8,128)(2,1)S(1)} %maximum_maximum_fusion), kind=kLoop, calls=%fused_computation.327 | loop fusion | bytes 14680064 | tf_op jit(solution)/shard_map/slice | solution.py:102
  135.6 51.0 %while.11 = (s32[]{:T(128)}, bf16[16,256,128]{2,1,0:T(8,128)(2,1)S(1)}, bf16[16,256,128]{1,2,0:T(8,128)(2,1)}, bf16[16,896,128]{1,2,0:T(8,128)(2,1)}, bf16[16,89...) while((s32[]{:T(128)}, ...), condition=%wide.region_9.10_spmd.clone, body=%wide.region_6.0_spmd.clone.sunk | while | flops 119995904 | bytes 3424237 | solution.py:119
  135.6 1.5 fusion.35
  137.4 1.3 fusion.37
  138.8 1.5 fusion.35
  140.6 1.3 fusion.37
  142.0 1.5 fusion.35
  143.8 1.3 fusion.37
  145.1 1.5 fusion.35
  147.0 1.3 fusion.37
  148.3 1.5 fusion.35
  150.2 1.3 fusion.37
  151.5 1.5 fusion.35
  153.4 1.3 fusion.37
  154.7 1.5 fusion.35
  156.6 1.3 fusion.37
  157.9 1.5 fusion.35
  159.8 1.3 fusion.37
  161.1 1.5 fusion.35
  162.9 1.3 fusion.37
  164.3 1.5 fusion.35
  166.1 1.3 fusion.37
  167.5 1.5 fusion.35
  169.3 1.3 fusion.37
  170.7 1.5 fusion.35
  172.5 1.3 fusion.37
  173.9 1.5 fusion.35
  175.7 1.3 fusion.37
  177.1 1.5 fusion.35
  178.9 1.3 fusion.37
  180.3 1.5 fusion.35
  182.1 1.3 fusion.37
  183.4 1.5 fusion.35
  185.3 1.3 fusion.37
  186.6 1.2 fusion.19
  187.9 35.5 %all-to-all-done = bf16[128,1,2,2,16,128]{5,4,3,2,1,0:T(8,128)(2,1)} async-done(((bf16[128,1,2,2,16,128]{5,4,3,2,1,0:T(8,128)(2,1)}), bf16[128,1,2,2,16,128]{5,4,3,2,1,0:T(8,128)(2,1)}, u32[]{:S(2)}, u32[]{:S(2)}) %all-to-all-start) | async-done | bytes 2097184 | tf_op jit(solution)/shard_map/all_to_all | solution.py:61
  223.4 3.3 %copy.44 = bf16[1,2,128,2,16,128]{5,4,3,2,1,0:T(8,128)(2,1)} copy(bf16[1,2,128,2,16,128]{5,4,3,1,0,2:T(8,128)(2,1)} %bitcast.144) | data formatting | bytes 4194304 | tf_op jit(solution)/shard_map/reshape | solution.py:60
  226.7 2.7 %gather_fusion = bf16[256,2,16,128]{3,2,1,0:T(8,128)(2,1)S(1)} fusion(bf16[2,256,16,128]{3,2,1,0:T(8,128)(2,1)} %bitcast.721, s32[1024]{0:T(1024)S(1)} %pad_clamp_fusion), kind=kCustom, calls=%fused_computation | custom fusion | bytes 4195328 | tf_op jit(solution)/shard_map/jit(_take)/gather | solution.py:64
  229.4 0.9 select_bitcast_fusion
  230.3 1.7 slice_bitcast_fusion
  (175 shorter events, 76.3 us)
Async XLA Ops:
  0.6 1.6 copy-start.1
  4.3 13.7 %copy-start = (bf16[256,2048]{1,0:T(8,128)(2,1)S(1)}, bf16[256,2048]{1,0:T(8,128)(2,1)}, u32[]{:S(2)}) copy-start(bf16[256,2048]{1,0:T(8,128)(2,1)} %param.11) | copy-start | bytes 3145732
  4.3 124.2 %collective-permute-start.2 = (bf16[2,256,2048]{1,2,0:T(8,128)(2,1)}, bf16[2,256,2048]{1,2,0:T(8,128)(2,1)}, u32[]{:S(2)}, u32[]{:S(2)}) collective-permute-start(bf16[2,256,2048]{1,2,0:T(8,128)(2,1)} %pad_maximum_fusion), channel_id=1, source_target_pairs={{0,1},{1,2},{2,3},{3,4},{4,5},{5,6},{6,7},{7,8},{8,9},{9,10},{10,1... | collective-permute-start | bytes 6291464 | tf_op jit(solution)/shard_map/ppermute | solution.py:16
  9.0 119.5 %collective-permute-start.1 = (bf16[2,256,2048]{1,2,0:T(8,128)(2,1)}, bf16[2,256,2048]{1,2,0:T(8,128)(2,1)}, u32[]{:S(2)}, u32[]{:S(2)}) collective-permute-start(bf16[2,256,2048]{1,2,0:T(8,128)(2,1)} %pad_maximum_fusion), channel_id=1, source_target_pairs={{0,2},{1,3},{2,4},{3,5},{4,6},{5,7},{6,8},{7,9},{8,10},{9,11},{10,... | collective-permute-start | bytes 6291464 | tf_op jit(solution)/shard_map/ppermute | solution.py:16
  14.7 113.8 %collective-permute-start = (bf16[2,128,2048]{1,2,0:T(8,128)(2,1)}, bf16[2,128,2048]{1,2,0:T(8,128)(2,1)}, u32[]{:S(2)}, u32[]{:S(2)}) collective-permute-start(bf16[2,128,2048]{1,2,0:T(8,128)(2,1)} %fusion.20), channel_id=1, source_target_pairs={{0,3},{1,4},{2,5},{3,6},{4,7},{5,8},{6,9},{7,10},{8,11},{9,12},{10... | collective-permute-start | bytes 3145736 | tf_op jit(solution)/shard_map/ppermute | solution.py:16
  96.1 28.1 %copy-start.5 = (s32[64]{0:T(128)S(1)}, s32[64]{0:T(128)}, u32[]{:S(2)}) copy-start(s32[64]{0:T(128)} %param.12) | copy-start | bytes 772
  96.1 28.2 %copy-start.2 = (s32[128]{0:T(128)S(1)}, s32[128]{0:T(128)}, u32[]{:S(2)}) copy-start(s32[128]{0:T(128)} %param.14) | copy-start | bytes 1540
  96.1 28.2 %copy-start.4 = (s32[128]{0:T(128)S(1)}, s32[128]{0:T(128)}, u32[]{:S(2)}) copy-start(s32[128]{0:T(128)} %param.13) | copy-start | bytes 1540
  96.1 29.1 %copy-start.3 = (s32[64]{0:T(128)S(1)}, s32[64]{0:T(128)}, u32[]{:S(2)}) copy-start(s32[64]{0:T(128)} %param.15) | copy-start | bytes 772
  96.2 127.2 %all-to-all-start = ((bf16[128,1,2,2,16,128]{5,4,3,2,1,0:T(8,128)(2,1)}), bf16[128,1,2,2,16,128]{5,4,3,2,1,0:T(8,128)(2,1)}, u32[]{:S(2)}, u32[]{:S(2)}) async-start(bf16[128,1,2,2,16,128]{5,4,3,2,1,0:T(8,128)(2,1)} %constant_dynamic-update-slice_fusion), calls=%async_computation | async-start | bytes 4194304 | tf_op jit(solution)/shard_map/all_to_all | solution.py:61
